TPU v7x, 32 devices: a whole 2x2x4 slice. The times are simulated.
32 devices in a mesh: left: 8 (over y, x, core), right: 4 (over z).
Axes of the slice: x: 2, y: 2, z: 4, core: 2. Of those that a mesh axis runs over, the one named last changes fastest.
Arguments:
- signal: float32 [256, 256, 1024], P(None, 'left', 'right'), may hold values from -6 to 6
- symbol_x: float32 [256], replicated, may hold values from 0.3 to 3
- symbol_y: float32 [256], replicated, may hold values from 0.3 to 3
- symbol_z: float32 [1024], replicated, may hold values from 0.3 to 3
Outputs:
- spectrum: float32 [128, 128, 512], P('left', 'right')
All inputs are finite; a program needn't handle non-finite values.
Results may differ from a plain program's by a relative error of at most 0.000096.
Values sent between devices are 32-bit elements; how exact they have to be, the bound alone decides.
A program may use at most 128 MiB of HBM per device.

v0:
```python
import jax
import jax.numpy as jnp
from jax import lax
from jax.sharding import PartitionSpec as P


def transform_table(count):
    rank = jnp.arange(count)
    angle = (
        jnp.pi
        / (4 * count)
        * ((2 * rank[:, None] + 1) * (2 * rank[None, :] + 1) % (8 * count)).astype(jnp.float32)
    )
    return jnp.cos(angle) * (2.0 / count) ** 0.5


def transform_dim(values, dim):
    moved = jnp.tensordot(
        values,
        transform_table(values.shape[dim]),
        axes=([dim], [0]),
        precision=lax.Precision.HIGHEST,
    )
    return jnp.moveaxis(moved, -1, dim)


def body(signal, symbol_x, symbol_y, symbol_z):
    part_values = signal
    part_values = transform_dim(part_values, 0)
    part_values = lax.slice_in_dim(part_values, 0, part_values.shape[0] // 2, axis=0)
    part_values = lax.all_to_all(part_values, "left", split_axis=0, concat_axis=1, tiled=True)
    part_values = transform_dim(part_values, 1)
    pencil_values = lax.slice_in_dim(part_values, 0, part_values.shape[1] // 2, axis=1)
    pencil_values = lax.all_to_all(pencil_values, "right", split_axis=1, concat_axis=2, tiled=True)
    pencil_values = transform_dim(pencil_values, 2)
    pencil_values = lax.slice_in_dim(pencil_values, 0, pencil_values.shape[2] // 2, axis=2)
    share_x = pencil_values.shape[0]
    part_x = lax.dynamic_slice_in_dim(symbol_x, lax.axis_index("left") * share_x, share_x)
    share_y = pencil_values.shape[1]
    part_y = lax.dynamic_slice_in_dim(symbol_y, lax.axis_index("right") * share_y, share_y)
    symbol = (
        part_x[:, None, None]
        + part_y[None, :, None]
        + symbol_z[: pencil_values.shape[2]][None, None, :]
    )
    pencil_values = pencil_values * ((1.0 - 0.2 * symbol) / (1.0 + 0.2 * symbol))
    return pencil_values


def solution(mesh):
    in_specs = (P(None, "left", "right"), P(), P(), P())
    out_specs = P("left", "right", None)
    return jax.shard_map(body, mesh=mesh, in_specs=in_specs, out_specs=out_specs, check_vma=False)
```

profile of v0, /device:TPU:0, one launch (start us, length us, event | category | flops | bytes accessed | tf_op | source)
XLA Modules:
  0.0 144.7 jit_solution(14525953596823520953)
XLA Ops:
  0.0 1.0 fusion.17
  1.0 13.0 %fusion = f32[128,32,256]{2,0,1:T(8,128)S(1)} fusion(f32[256,32,256]{2,1,0:T(8,128)} %param.4, f32[256,256,1]{1,0,2:T(8,128)S(1)} %fusion.17), kind=kOutput, calls=%fused_computation | convolution fusion | flops 3221225472 | bytes 12713984 | tf_op jit(solution)/shard_map/dot_general | solution.py:18
  14.1 2.4 %copy.24 = f32[128,32,256]{2,1,0:T(8,128)S(1)} copy(f32[128,32,256]{2,0,1:T(8,128)S(1)} %fusion) | data formatting | bytes 8388608 | tf_op jit(solution)/shard_map/slice | solution.py:30
  16.5 54.0 %all_to_all.36 = f32[128,32,256]{2,1,0:T(8,128)S(1)} all-to-all(f32[128,32,256]{2,1,0:T(8,128)S(1)} %copy.24), channel_id=1, replica_groups=mesh['left'=8,'right'=4] {'left'}, dimensions={0} | all-to-all | bytes 8388608 | tf_op jit(solution)/shard_map/all_to_all | solution.py:31
  70.5 0.6 copy.25
  71.1 7.6 %convolution_bitcast_fusion = f32[16,256,256]{1,2,0:T(8,128)S(1)} fusion(f32[16,256,256]{2,1,0:T(8,128)S(1)} %bitcast.17, s32[256]{0:T(256)S(1)} %multiply_add_fusion.1), kind=kOutput, calls=%fused_computation.13 | convolution fusion | flops 3222208512 | bytes 8389632 | tf_op jit(solution)/shard_map/dot_general | solution.py:18
  78.7 0.2 slice.19
  78.9 0.0 copy-start
  78.9 0.0 copy-start.1
  78.9 2.1 %copy.27 = f32[16,128,256]{2,0,1:T(8,128)} copy(f32[16,128,256]{1,2,0:T(8,128)S(1)} %slice.19) | data formatting | bytes 4194304 | tf_op jit(solution)/shard_map/slice | solution.py:33
  81.0 4.9 %all-to-all-start.1 = ((f32[16,128,256]{2,0,1:T(8,128)}), f32[16,128,256]{2,0,1:T(8,128)S(1)}, u32[]{:S(2)}, u32[]{:S(2)}) async-start(f32[16,128,256]{2,0,1:T(8,128)} %copy.27), calls=%async_computation.1 | async-start | bytes 4194304 | tf_op jit(solution)/shard_map/all_to_all | solution.py:34
  85.8 0.0 copy-done
  85.8 0.1 dynamic_slice.7
  85.9 0.0 copy-done.1
  85.9 0.1 dynamic_slice.6
  86.0 0.1 broadcast_add_fusion
  86.1 16.7 %fusion.6 = f32[1024,1024,1]{1,0,2:T(8,128)} fusion(s32[1024]{0:T(1024)S(1)} %multiply_add_fusion), kind=kLoop, calls=%fused_computation.11 | loop fusion | flops 15728640 | bytes 4198400 | tf_op jit(solution)/shard_map/mul | solution.py:14
  102.8 30.7 %all-to-all-done.1 = f32[16,128,256]{2,0,1:T(8,128)S(1)} async-done(((f32[16,128,256]{2,0,1:T(8,128)}), f32[16,128,256]{2,0,1:T(8,128)S(1)}, u32[]{:S(2)}, u32[]{:S(2)}) %all-to-all-start.1) | async-done | bytes 2097184 | tf_op jit(solution)/shard_map/all_to_all | solution.py:34
  133.5 0.0 slice-start
  133.5 2.7 %copy.29 = f32[16,32,4,256]{3,2,1,0:T(4,128)} copy(f32[16,32,4,256]{3,0,1,2:T(8,128)S(1)} %bitcast.19) | data formatting | bytes 4194304 | tf_op jit(solution)/shard_map/all_to_all | solution.py:34
  136.2 2.3 %all_to_all.33 = f32[16,32,1024]{2,1,0:T(8,128)S(1)} reshape(f32[16,32,4,256]{3,2,1,0:T(4,128)} %copy.29) | data formatting | bytes 4194304 | tf_op jit(solution)/shard_map/all_to_all | solution.py:34
  138.5 0.0 slice-done
  138.5 6.2 %fusion.10 = f32[16,32,512]{2,1,0:T(8,128)} fusion(f32[16,32,1024]{2,1,0:T(8,128)S(1)} %all_to_all.33, f32[1024,1024,1]{1,0,2:T(8,128)} %fusion.6, f32[512]{0:T(512)S(1)} %slice-done, f32[16,32]{1,0:T(8,128)S(1)} %broadcast_add_fusion), kind=kOutput, calls=%fused_computation.16 | convolution fusion | flops 3222798336 | bytes 5246976 | tf_op jit(solution)/shard_map/dot_general | solution.py:18
  (2 shorter events, 0.0 us)
Async XLA Ops:
  78.9 7.0 %copy-start = (f32[256]{0:T(256)S(1)}, f32[256]{0:T(256)}, u32[]{:S(2)}) copy-start(f32[256]{0:T(256)} %param.6) | copy-start | bytes 3076
  78.9 7.0 %copy-start.1 = (f32[256]{0:T(256)S(1)}, f32[256]{0:T(256)}, u32[]{:S(2)}) copy-start(f32[256]{0:T(256)} %param.5) | copy-start | bytes 3076
  81.0 52.5 %all-to-all-start.1 = ((f32[16,128,256]{2,0,1:T(8,128)}), f32[16,128,256]{2,0,1:T(8,128)S(1)}, u32[]{:S(2)}, u32[]{:S(2)}) async-start(f32[16,128,256]{2,0,1:T(8,128)} %copy.27), calls=%async_computation.1 | async-start | bytes 4194304 | tf_op jit(solution)/shard_map/all_to_all | solution.py:34
  133.5 5.0 %slice-start = ((f32[1024]{0:T(1024)}), f32[512]{0:T(512)S(1)}, s32[]{:S(2)}) async-start(f32[1024]{0:T(1024)} %param.7), calls=%async_computation.2 | async-start | bytes 4096 | tf_op jit(solution)/shard_map/slice | solution.py:44
where the time goes:
time: 145 us
  blocking collectives  54 us (37%)
  waiting for transfers between devices  30.7 us (21%)
  matrix products  26.8 us (18%)
  other arithmetic  17.8 us (12%)
  local copies, waits for them, and re-layouts  10.4 us (7%)
  starting transfers between devices  4.87 us (3%)
    all_to_all x1, blocking collectives, body(): lax.all_to_all(part_values, 'left', split_axis=0, concat_axis=1, tiled=True)  54 us
    all_to_all x1, waiting for transfers between devices, body(): lax.all_to_all(pencil_values, 'right', split_axis=1, concat_axis=2, tiled...  30.7 us
    dot_general x3, matrix products, transform_dim(): jnp.tensordot(values, transform_table(values.shape[dim]), axes=([dim], [0...  26.8 us
    mul x2, other arithmetic, transform_table(): return jnp.cos(angle) * (2.0 / count) ** 0.5  17.7 us
    all_to_all x2, local copies, waits for them, and re-layouts, body(): lax.all_to_all(pencil_values, 'right', split_axis=1, concat_axis=2, tiled...  5 us
    all_to_all x1, starting transfers between devices, body(): lax.all_to_all(pencil_values, 'right', split_axis=1, concat_axis=2, tiled...  4.87 us
  transfers between devices with their start and end apart: 1, of which 1 were waited for; matrix products, arithmetic and copies ran while one was open for 12% of the time, Pallas kernels for 0%

commit v1 on v0

--- a/solution.py
+++ b/solution.py
@@ -31,7 +31,9 @@
     part_values = lax.all_to_all(part_values, "left", split_axis=0, concat_axis=1, tiled=True)
     part_values = transform_dim(part_values, 1)
     pencil_values = lax.slice_in_dim(part_values, 0, part_values.shape[1] // 2, axis=1)
-    pencil_values = lax.all_to_all(pencil_values, "right", split_axis=1, concat_axis=2, tiled=True)
+    cells = jnp.split(pencil_values, lax.axis_size("right"), axis=1)
+    incoming = lax.all_to_all(jnp.stack(cells), "right", 0, 0)
+    pencil_values = jnp.concatenate(incoming, axis=2)
     pencil_values = transform_dim(pencil_values, 2)
     pencil_values = lax.slice_in_dim(pencil_values, 0, pencil_values.shape[2] // 2, axis=2)
     share_x = pencil_values.shape[0]

time: 145 us -> 137 us (0.945)
  local copies, waits for them, and re-layouts: 10.4 us -> 5.48 us
  matrix products: 26.8 us -> 22.6 us
  other arithmetic: 17.8 us -> 19.3 us
    all_to_all x2 -> x0, local copies, waits for them, and re-layouts: 5 us -> none  [body(): lax.all_to_all(pencil_values, 'right', split_axis=1, concat_axis=2, tiled...]
    dot_general x3, matrix products: 26.8 us -> 22.6 us  [transform_dim(): jnp.tensordot(values, transform_table(values.shape[dim]), axes=([dim], [0...]
    slice x2 -> x0, local copies, waits for them, and re-layouts: 2.24 us -> none  [body(): lax.slice_in_dim(part_values, 0, part_values.shape[1] // 2, axis=1)]
    unnamed x4 -> x6, local copies, waits for them, and re-layouts: 0.01 us -> 1.88 us
    another operation x0 -> x1, other arithmetic: none -> 1.47 us  [body(): incoming = lax.all_to_all(jnp.stack(cells), 'right', 0, 0)]
where the time goes in v1:
time: 137 us
  blocking collectives  54 us (39%)
  waiting for transfers between devices  30.7 us (22%)
  matrix products  22.6 us (16%)
  other arithmetic  19.3 us (14%)
  local copies, waits for them, and re-layouts  5.48 us (4%)
  starting transfers between devices  4.87 us (4%)
    all_to_all x1, blocking collectives, body(): lax.all_to_all(part_values, 'left', split_axis=0, concat_axis=1, tiled=True)  54 us
    all_to_all x1, waiting for transfers between devices, body(): incoming = lax.all_to_all(jnp.stack(cells), 'right', 0, 0)  30.7 us
    dot_general x3, matrix products, transform_dim(): jnp.tensordot(values, transform_table(values.shape[dim]), axes=([dim], [0...  22.6 us
    mul x2, other arithmetic, transform_table(): return jnp.cos(angle) * (2.0 / count) ** 0.5  17.7 us
    all_to_all x1, starting transfers between devices, body(): incoming = lax.all_to_all(jnp.stack(cells), 'right', 0, 0)  4.87 us
  transfers between devices with their start and end apart: 1, of which 1 were waited for; matrix products, arithmetic and copies ran while one was open for 12% of the time, Pallas kernels for 0%

profile of v1, /device:TPU:0, one launch (start us, length us, event | category | flops | bytes accessed | tf_op | source)
XLA Modules:
  0.0 137.0 jit_solution(2609912275605393516)
XLA Ops:
  0.0 1.0 fusion.17
  1.0 13.0 %fusion = f32[128,32,256]{2,0,1:T(8,128)S(1)} fusion(f32[256,32,256]{2,1,0:T(8,128)} %param.4, f32[256,256,1]{0,1,2:T(8,128)S(1)} %fusion.17), kind=kOutput, calls=%fused_computation | convolution fusion | flops 3221225472 | bytes 12713984 | tf_op jit(solution)/shard_map/dot_general | solution.py:18
  14.0 2.4 %copy.11 = f32[128,32,256]{2,1,0:T(8,128)S(1)} copy(f32[128,32,256]{2,0,1:T(8,128)S(1)} %fusion) | data formatting | bytes 8388608 | tf_op jit(solution)/shard_map/slice | solution.py:30
  16.5 54.0 %all_to_all.23 = f32[128,32,256]{2,1,0:T(8,128)S(1)} all-to-all(f32[128,32,256]{2,1,0:T(8,128)S(1)} %copy.11), channel_id=1, replica_groups=mesh['left'=8,'right'=4] {'left'}, dimensions={0} | all-to-all | bytes 8388608 | tf_op jit(solution)/shard_map/all_to_all | solution.py:31
  70.5 0.6 copy.12
  71.1 5.0 %convolution_bitcast_fusion = f32[16,256,256]{2,1,0:T(8,128)S(1)} fusion(f32[16,256,256]{2,1,0:T(8,128)S(1)} %bitcast.24, s32[256]{0:T(256)S(1)} %multiply_add_fusion.1), kind=kOutput, calls=%fused_computation.13 | convolution fusion | flops 3222208512 | bytes 8389632 | tf_op jit(solution)/shard_map/dot_general | solution.py:18
  76.1 0.1 slice_bitcast_fusion.3
  76.2 0.0 copy-start.1
  76.3 0.0 copy-start.2
  76.3 1.5 %pad_maximum_fusion = f32[4,16,32,256]{3,2,1,0:T(8,128)} fusion(f32[1,16,32,256]{3,2,1,0:T(8,128)S(1)} %get-tuple-element.6, f32[1,16,32,256]{3,2,1,0:T(8,128)S(1)} %get-tuple-element.7, f32[1,16,32,256]{3,2,1,0:T(8,128)S(1)} %get-tuple-element.8, f32[1,16,32,256]{3,2,1,0:T(8,128)S(1)} %get-tuple-element.5), kind=kLoop, calls=%fused_computation.16 | loop fusion | flops 1572864 | bytes 4194304 | tf_op jit(solution)/shard_map/stack | solution.py:35
  77.7 4.9 %all-to-all-start.1 = ((f32[4,16,32,256]{3,2,1,0:T(8,128)}), f32[4,16,32,256]{3,2,1,0:T(8,128)S(1)}, u32[]{:S(2)}, u32[]{:S(2)}) async-start(f32[4,16,32,256]{3,2,1,0:T(8,128)} %pad_maximum_fusion), calls=%async_computation.1 | async-start | bytes 4194304 | tf_op jit(solution)/shard_map/all_to_all | solution.py:35
  82.6 0.0 copy-done.1
  82.6 0.1 dynamic_slice.6
  82.7 0.0 copy-done.2
  82.7 0.1 dynamic_slice.7
  82.8 0.1 broadcast_add_fusion
  82.8 0.0 slice-start
  82.8 16.7 %fusion.6 = f32[1024,1024,1]{1,0,2:T(8,128)} fusion(s32[1024]{0:T(1024)S(1)} %multiply_add_fusion), kind=kLoop, calls=%fused_computation.11 | loop fusion | flops 15728640 | bytes 4198400 | tf_op jit(solution)/shard_map/mul | solution.py:14
  99.5 30.7 %all-to-all-done.1 = f32[4,16,32,256]{3,2,1,0:T(8,128)S(1)} async-done(((f32[4,16,32,256]{3,2,1,0:T(8,128)}), f32[4,16,32,256]{3,2,1,0:T(8,128)S(1)}, u32[]{:S(2)}, u32[]{:S(2)}) %all-to-all-start.1) | async-done | bytes 2097184 | tf_op jit(solution)/shard_map/all_to_all | solution.py:35
  130.3 0.0 copy-start
  130.3 0.3 copy.14
  130.6 0.0 slice-done
  130.6 1.9 %copy-done = f32[1024,1024,1]{1,0,2:T(8,128)S(1)} copy-done((f32[1024,1024,1]{1,0,2:T(8,128)S(1)}, f32[1024,1024,1]{1,0,2:T(8,128)}, u32[]{:S(2)}) %copy-start) | copy-done | bytes 4194328
  132.4 4.6 %fusion.10 = f32[16,32,512]{2,1,0:T(8,128)} fusion(f32[16,32,1024]{2,1,0:T(8,128)S(1)} %bitcast.27, f32[1024,1024,1]{1,0,2:T(8,128)S(1)} %copy-done, f32[512]{0:T(512)S(1)} %slice-done, f32[16,32]{1,0:T(8,128)S(1)} %broadcast_add_fusion), kind=kOutput, calls=%fused_computation.17 | convolution fusion | flops 3222798336 | bytes 5253120 | tf_op jit(solution)/shard_map/dot_general | solution.py:18
  (2 shorter events, 0.0 us)
Async XLA Ops:
  76.2 6.4 %copy-start.1 = (f32[256]{0:T(256)S(1)}, f32[256]{0:T(256)}, u32[]{:S(2)}) copy-start(f32[256]{0:T(256)} %param.5) | copy-start | bytes 3076
  76.3 6.4 %copy-start.2 = (f32[256]{0:T(256)S(1)}, f32[256]{0:T(256)}, u32[]{:S(2)}) copy-start(f32[256]{0:T(256)} %param.6) | copy-start | bytes 3076
  77.7 52.5 %all-to-all-start.1 = ((f32[4,16,32,256]{3,2,1,0:T(8,128)}), f32[4,16,32,256]{3,2,1,0:T(8,128)S(1)}, u32[]{:S(2)}, u32[]{:S(2)}) async-start(f32[4,16,32,256]{3,2,1,0:T(8,128)} %pad_maximum_fusion), calls=%async_computation.1 | async-start | bytes 4194304 | tf_op jit(solution)/shard_map/all_to_all | solution.py:35
  82.8 47.7 %slice-start = ((f32[1024]{0:T(1024)}), f32[512]{0:T(512)S(1)}, s32[]{:S(2)}) async-start(f32[1024]{0:T(1024)} %param.7), calls=%async_computation.2 | async-start | bytes 4096 | tf_op jit(solution)/shard_map/slice | solution.py:46
  130.3 2.2 %copy-start = (f32[1024,1024,1]{1,0,2:T(8,128)S(1)}, f32[1024,1024,1]{1,0,2:T(8,128)}, u32[]{:S(2)}) copy-start(f32[1024,1024,1]{1,0,2:T(8,128)} %fusion.6) | copy-start | bytes 12582916
